TPU v7x, 128 devices: a whole 4x4x4 slice. The times are simulated.
128 devices in a mesh: rep: 8 (over z, core), ep: 16 (over x, y).
Axes of the slice: x: 4, y: 4, z: 4, core: 2. Of those that a mesh axis runs over, the one named last changes fastest.
Arguments:
- latent_pages: bfloat16 [6144, 36864], P(('rep', 'ep')), may hold values from -4 to 4
- queries: bfloat16 [1024, 147456], P(('rep', 'ep')), may hold values from -4 to 4
- residual: bfloat16 [1024, 14336], P(('rep', 'ep')), may hold values from -6 to 6
- page_count: int32 [8, 16, 8], P(None, 'ep'), may hold values from 1 to 12, 48 in all within a row
- last_fill: int32 [8, 16, 8], P(None, 'ep'), may hold values from 4 to 64
- page_order: int32 [128, 48], P(('rep', 'ep')), may hold values from 0 to 47, each once within a row
- shed_slots: int32 [8, 16, 2], P(None, 'ep'), may hold values from 0 to 7, as said below
- shed_shift: int32 [16, 2], P('ep'), may hold values from 1 to 7
- expert_ids: int32 [4096, 8], P(('rep', 'ep')), may hold values from 0 to 127, all different within a row; in each aligned block of 32 rows (0 to 31, 32 to 63, ...) at most 4 rows name the same one
- gate_weight: float32 [4096, 8], P(('rep', 'ep')), may hold values from 0.05 to 0.5
- expert_home: int32 [128], replicated, may hold values from 0 to 127, each once
- norm_gain: float32 [3584], replicated, may hold values from 0.1 to 1.9
- value_up: bfloat16 [64, 512, 128], P('ep'), may hold values from -0.59765625 to 0.59765625
- out_weight: bfloat16 [8192, 3584], P('ep'), may hold values from -0.14941406 to 0.14941406
- expert_in: bfloat16 [128, 3584, 1024], P(('rep', 'ep')), may hold values from -0.09375 to 0.09375
- expert_out: bfloat16 [128, 1024, 3584], P(('rep', 'ep')), may hold values from -0.1875 to 0.1875
Outputs:
- attn_proj: bfloat16 [1024, 14336], P(('rep', 'ep'))
- layer_out: bfloat16 [1024, 14336], P(('rep', 'ep'))
Inputs may be any that keep to these rules, and one draw needn't show every extreme that they name: `shed_slots`: for each device, 2 different slots. `expert_ids`: each row names 8 different experts; in the rows of one device no expert is named by more than 4 rows.
All inputs are finite; a program needn't handle non-finite values.
Results may differ from a plain program's by a relative error of at most 0.015.
Values may be sent and summed in bfloat16 or wider, within the bound.
No kernel may reach another device: no remote copies, remote signals or barrier semaphores. Data moves between devices by JAX's collectives and lax.ppermute only.
A program may use at most 192 MiB of HBM per device.

v0:
```python
import jax
import jax.numpy as jnp
from jax import lax
from jax.sharding import Mesh
from jax.sharding import PartitionSpec as P

D = 3584
HEADS = 64
LAT = 512
KVW = 576
VHEAD = 128
TOP = 8
PAGE = 64
SPEC = 4
MAXP = 12
REQ_DEV = 8
PAGES_DEV = 48
EP = ("ep_0", "ep_1")
REP_EP = ("rep", "ep_0", "ep_1")


SCORE_SCALE = 192.0 ** (-0.5)
NORM_EPS = 0.25


def shifted(value, axis, steps):
    count = lax.axis_size(axis)
    pairs = [(source, (source + steps) % count) for source in range(count)]
    return lax.ppermute(value, axis, pairs)


def own_rows_2(terms, axes):
    so_far = terms.astype(jnp.bfloat16)
    for axis in axes:
        so_far = lax.psum_scatter(so_far, axis, scatter_dimension=0, tiled=True)
    return so_far.astype(jnp.float32)


def attend(key_block, query_block, lengths):
    request_count = key_block.shape[0]
    key_rows = key_block.reshape(request_count, MAXP * PAGE, KVW)
    query_rows = query_block.reshape(request_count, SPEC * HEADS, KVW)
    scores = (
        jnp.einsum("rqc,rkc->rqk", query_rows, key_rows, preferred_element_type=jnp.float32)
        * SCORE_SCALE
    )
    position = jnp.arange(MAXP * PAGE, dtype=jnp.int32)
    offset = jnp.arange(SPEC * HEADS, dtype=jnp.int32) // HEADS
    visible_end = lengths[:, None] - SPEC + 1 + offset[None, :]
    visible = position[None, None, :] < visible_end[:, :, None]
    scores = jnp.where(visible, scores, -1e30)
    exponent = jnp.exp(scores - jnp.max(scores, axis=2, keepdims=True))
    probability = (exponent / jnp.sum(exponent, axis=2, keepdims=True)).astype(jnp.bfloat16)
    latent = jnp.einsum(
        "rqk,rkl->rql", probability, key_rows[:, :, :LAT], preferred_element_type=jnp.float32
    )
    return latent.astype(jnp.bfloat16).reshape(request_count, SPEC * HEADS * LAT)


def fill_slots(arrived, picker, present, own_rows):
    return jnp.where(present[:, None], arrived[picker], own_rows)


def per_device(
    latent_pages,
    queries,
    residual,
    page_count,
    last_fill,
    page_order,
    shed_slots,
    shed_shift,
    expert_ids,
    gate_weight,
    expert_home,
    norm_gain,
    value_up,
    out_weight,
    expert_in,
    expert_out,
):
    rep_count = lax.axis_size("rep")
    col_count = lax.axis_size(EP)
    device_count = rep_count * col_count
    replica = lax.axis_index("rep")
    lengths = (page_count[:, 0, :] - 1) * PAGE + last_fill[:, 0, :]
    shed_table = shed_slots[:, 0, :]
    own_counts = page_count[replica, 0, :]
    offsets = jnp.cumsum(own_counts) - own_counts
    page_steps = jnp.arange(MAXP, dtype=jnp.int32)
    positions = jnp.minimum(offsets[:, None] + page_steps[None, :], PAGES_DEV - 1)
    own_keys = latent_pages[page_order[0][positions]].reshape(REQ_DEV, MAXP * PAGE * KVW)
    own_lengths = lengths[replica]
    own_sheds = shed_table[replica]
    shifts = shed_shift[0]
    matches = own_sheds[None, :] == jnp.arange(REQ_DEV, dtype=jnp.int32)[:, None]
    present = jnp.any(matches, axis=1)
    picker = jnp.argmax(matches, axis=1)
    latent_width = SPEC * HEADS * LAT
    own_latent = attend(own_keys, queries, own_lengths)
    arrived = jnp.concatenate((own_latent[own_sheds], residual[own_sheds]), axis=1)
    for bit_level in range(rep_count.bit_length() - 1):
        moved = shifted(arrived, "rep", 1 << bit_level)
        taking = shifts // (1 << bit_level) % 2 == 1
        arrived = jnp.where(taking[:, None], moved, arrived)
    latent_all = fill_slots(arrived[:, :latent_width], picker, present, own_latent)
    served_rest = fill_slots(arrived[:, latent_width:], picker, present, residual)
    tokens_dev = REQ_DEV * SPEC
    heads_dev = value_up.shape[0]
    token_latent = latent_all.reshape(tokens_dev, HEADS * LAT)
    regrouped = lax.all_to_all(token_latent, EP, split_axis=1, concat_axis=0, tiled=True)
    row_block = regrouped.reshape(tokens_dev * lax.axis_size(EP), heads_dev, LAT)
    lifted = jnp.einsum(
        "thl,hlv->thv", row_block, value_up, preferred_element_type=jnp.float32
    ).astype(jnp.bfloat16)
    branch = own_rows_2(
        jnp.dot(
            lifted.reshape(tokens_dev * lax.axis_size(EP), heads_dev * VHEAD),
            out_weight,
            preferred_element_type=jnp.float32,
        ),
        EP,
    )
    mixed = served_rest.reshape(tokens_dev, D).astype(jnp.float32) + branch
    square = jnp.mean(mixed * mixed, axis=1, keepdims=True)
    normed = (mixed * lax.rsqrt(square + NORM_EPS) * norm_gain).astype(jnp.bfloat16)
    capacity = max(4, 2 * tokens_dev * TOP // device_count)
    flat_ids = expert_ids.reshape(-1)
    target = expert_home[flat_ids]
    hits = (target[:, None] == jnp.arange(device_count, dtype=jnp.int32)[None, :]).astype(jnp.int32)
    before = jnp.sum((jnp.cumsum(hits, axis=0) - hits) * hits, axis=1)
    slot_index = target * capacity + before
    buffer_rows = jnp.arange(device_count * capacity, dtype=jnp.int32)
    landing = buffer_rows[:, None, None] == slot_index.reshape(tokens_dev, TOP)[None, :, :]
    chooser = jnp.any(landing, axis=2).astype(jnp.bfloat16)
    outgoing_tokens = jnp.dot(chooser, normed, preferred_element_type=jnp.float32).astype(
        jnp.bfloat16
    )
    incoming = lax.all_to_all(
        outgoing_tokens.reshape(device_count, capacity, D),
        REP_EP,
        split_axis=0,
        concat_axis=0,
        tiled=True,
    )
    inner_act = jax.nn.silu(
        jnp.dot(
            incoming.reshape(device_count * capacity, D),
            expert_in[0],
            preferred_element_type=jnp.float32,
        )
    ).astype(jnp.bfloat16)
    outer_out = jnp.dot(inner_act, expert_out[0], preferred_element_type=jnp.float32).astype(
        jnp.bfloat16
    )
    returned = lax.all_to_all(
        outer_out.reshape(device_count, capacity, D),
        REP_EP,
        split_axis=0,
        concat_axis=0,
        tiled=True,
    )
    picked = (
        returned.reshape(device_count * capacity, D)[slot_index]
        .reshape(tokens_dev, TOP, D)
        .astype(jnp.float32)
    )
    moe_sum = jnp.sum(gate_weight[:, :, None] * picked, axis=1)
    attn_proj = branch.astype(jnp.bfloat16).reshape(REQ_DEV, SPEC * D)
    layer_out = (mixed + moe_sum).astype(jnp.bfloat16).reshape(REQ_DEV, SPEC * D)
    return (attn_proj, layer_out)


def solution(mesh):
    torus = Mesh(mesh.devices.reshape(mesh.shape["rep"], 4, 4), ("rep", "ep_0", "ep_1"))
    return jax.shard_map(
        per_device,
        mesh=torus,
        in_specs=(
            P(REP_EP, None),
            P(REP_EP, None),
            P(REP_EP, None),
            P(None, EP, None),
            P(None, EP, None),
            P(REP_EP, None),
            P(None, EP, None),
            P(EP, None),
            P(REP_EP, None),
            P(REP_EP, None),
            P(),
            P(),
            P(EP, None, None),
            P(EP, None),
            P(REP_EP, None, None),
            P(REP_EP, None, None),
        ),
        out_specs=(P(REP_EP, None), P(REP_EP, None)),
        check_vma=False,
    )
```

profile of v0, /device:TPU:1, one launch (start us, length us, event | category | flops | bytes accessed | tf_op | source)
XLA Modules:
  0.0 409.3 jit_solution(7821792258166514512)
XLA Ops:
  7.2 0.6 and_select_fusion
  7.8 1.0 fusion.45
  8.8 0.2 reduce-window.18
  9.0 0.7 bitcast_subtract_fusion.1
  9.8 1.6 gather_fusion
  11.6 8.1 %gather_fusion.1 = bf16[96,36864]{1,0:T(8,128)(2,1)} fusion(bf16[48,36864]{1,0:T(8,128)(2,1)S(1)} %copy-done, s32[1024]{0:T(1024)S(1)} %pad_clamp_fusion.4), kind=kCustom, calls=%fused_computation.1 | custom fusion | bytes 14156160 | tf_op jit(solution)/shard_map/gather | solution.py:92
  19.7 14.3 %reshape_reshape.3 = bf16[8,768,576]{2,1,0:T(8,128)(2,1)} reshape(bf16[96,36864]{1,0:T(8,128)(2,1)} %gather_fusion.1) | data formatting | bytes 14155776 | tf_op jit(solution)/shard_map/reshape;reshape | solution.py:41
  34.0 2.7 reshape.532
  36.7 3.3 reshape.428
  40.1 10.7 %fusion.52 = (f32[8,256]{1,0:T(8,128)S(1)}, f32[8,256,768]{1,2,0:T(8,128)}) fusion(s32[8,256]{1,0:T(8,128)S(1)} %broadcast_add_fusion.1, bf16[8,768,576]{2,1,0:T(8,128)(2,1)} %reshape_reshape.3, bf16[8,256,576]{2,1,0:T(8,128)(2,1)} %reshape.428), kind=kOutput, calls=%fused_computation.120 | convolution fusion | flops 1819804416 | bytes 15745024 | tf_op jit(solution)/shard_map/sub | solution.py:52
  50.8 6.4 %fusion.18 = bf16[8,256,512]{2,1,0:T(8,128)(2,1)S(1)} fusion(bf16[8,768,576]{2,1,0:T(8,128)(2,1)} %reshape_reshape.3, f32[8,256,768]{1,2,0:T(8,128)} %get-tuple-element.14, f32[8,256]{1,0:T(8,128)S(1)} %get-tuple-element.13), kind=kOutput, calls=%fused_computation.36 | convolution fusion | flops 1614807040 | bytes 14688256 | tf_op jit(solution)/shard_map/rqk,rkl->rql/dot_general | solution.py:54
  57.3 1.2 copy.49
  58.8 0.2 dynamic-slice_reduce_fusion
  59.2 0.9 gather_fusion.6
  60.1 0.2 constant_dynamic-update-slice_fusion.2
  60.3 0.9 gather_fusion.7
  61.2 0.6 gather_fusion.2
  61.8 0.2 constant_dynamic-update-slice_fusion.1
  62.1 3.0 collective-permute-start
  65.1 6.7 %collective-permute-done = bf16[2,145408]{1,0:T(2,128)(2,1)S(1)} collective-permute-done((bf16[2,145408]{1,0:T(2,128)(2,1)S(1)}, bf16[2,145408]{1,0:T(2,128)(2,1)S(1)}, u32[]{:S(2)}, u32[]{:S(2)}) %collective-permute-start) | collective-permute-done | bytes 581664 | tf_op jit(solution)/shard_map/ppermute | solution.py:29
  71.8 0.8 broadcast_select_fusion
  72.6 1.7 collective-permute-start.1
  74.3 11.6 %collective-permute-done.1 = bf16[2,145408]{1,0:T(2,128)(2,1)S(1)} collective-permute-done((bf16[2,145408]{1,0:T(2,128)(2,1)S(1)}, bf16[2,145408]{1,0:T(2,128)(2,1)S(1)}, u32[]{:S(2)}, u32[]{:S(2)}) %collective-permute-start.1) | collective-permute-done | bytes 581664 | tf_op jit(solution)/shard_map/ppermute | solution.py:29
  85.9 1.0 broadcast_select_fusion.1
  86.9 3.6 collective-permute-start.2
  90.7 3.1 reshape.430
  93.9 0.6 iota_reduce_fusion
  94.6 6.4 %collective-permute-done.2 = bf16[2,145408]{1,0:T(2,128)(2,1)} collective-permute-done((bf16[2,145408]{1,0:T(2,128)(2,1)S(1)}, bf16[2,145408]{1,0:T(2,128)(2,1)}, u32[]{:S(2)}, u32[]{:S(2)}) %collective-permute-start.2) | collective-permute-done | bytes 581664 | tf_op jit(solution)/shard_map/ppermute | solution.py:29
  101.0 1.8 broadcast_select_fusion.2
  102.8 0.8 copy-done.7
  103.6 0.4 fusion.51
  104.0 2.2 gather_fusion.8
  106.2 2.2 gather_fusion.9
  108.4 3.0 pad_maximum_fusion
  111.4 3.8 gather.34
  115.3 6.0 %copy_select_fusion = bf16[32,16,2048]{2,0,1:T(8,128)(2,1)S(1)} fusion(bf16[32,16,2048]{2,1,0:T(8,128)(2,1)S(1)} %reshape.430, bf16[32,16,2048]{2,1,0:T(8,128)(2,1)} %gather.34, pred[32]{0:T(512)(128)(4,1)S(1)} %broadcast_in_dim.45), kind=kLoop, calls=%fused_computation.34 | loop fusion | flops 1048576 | bytes 6291488 | tf_op jit(solution)/shard_map/jit(_where)/select_n | solution.py:61
  121.3 30.6 %all_to_all.23 = bf16[32,16,2048]{2,0,1:T(8,128)(2,1)S(1)} all-to-all(bf16[32,16,2048]{2,0,1:T(8,128)(2,1)S(1)} %copy_select_fusion), channel_id=1, replica_groups=mesh['rep'=8,'ep_0'=4,'ep_1'=4] {'ep_0','ep_1'}, dimensions={1} | all-to-all | bytes 4194304 | tf_op jit(solution)/shard_map/all_to_all | solution.py:111
  151.9 2.8 reshape.431
  154.7 2.6 fusion.23
  157.4 3.9 convolution_convert_fusion.1
  161.4 0.6 copy-done.2
  161.9 2.3 gather_fusion.4
  164.3 0.2 fusion.31
  164.9 0.2 fusion.28
  165.2 0.9 slice.43
  166.0 0.7 gather_fusion.3
  166.7 40.7 %reduce-scatter.3.cloned.1.call-done = bf16[128,3584]{1,0:T(8,128)(2,1)} async-done(((bf16[512,3584]{1,0:T(8,128)(2,1)}), bf16[128,3584]{1,0:T(8,128)(2,1)}) %reduce-scatter.3.cloned.1.call-update) | async-done | bytes 917520 | tf_op jit(solution)/shard_map/reduce_scatter | solution.py:35
  207.7 23.9 %reduce-scatter.5.cloned.1.call-done = bf16[32,3584]{1,0:T(8,128)(2,1)} async-done(((bf16[128,3584]{1,0:T(8,128)(2,1)}), bf16[32,3584]{1,0:T(8,128)(2,1)}) %reduce-scatter.5.cloned.1.call-update) | async-done | bytes 229392 | tf_op jit(solution)/shard_map/reduce_scatter | solution.py:35
  231.6 1.1 multiply_reduce_fusion
  232.7 4.0 convolution_convert_fusion
  236.6 7.0 %reshape.436 = bf16[128,4,3584]{2,1,0:T(4,128)(2,1)} reshape(bf16[512,3584]{1,0:T(8,128)(2,1)} %convolution_convert_fusion) | data formatting | bytes 7340032 | tf_op jit(solution)/shard_map/reshape | solution.py:140
  243.6 56.3 %all_to_all.24 = bf16[128,4,3584]{2,1,0:T(4,128)(2,1)} all-to-all(bf16[128,4,3584]{2,1,0:T(4,128)(2,1)} %reshape.436), channel_id=1, replica_groups=mesh['rep'=8,'ep_0'=4,'ep_1'=4] {'rep','ep_0','ep_1'}, dimensions={0} | all-to-all | bytes 7340032 | tf_op jit(solution)/shard_map/all_to_all | solution.py:139
  300.0 6.7 %reshape.437 = bf16[512,3584]{1,0:T(8,128)(2,1)} reshape(bf16[128,4,3584]{2,1,0:T(4,128)(2,1)} %all_to_all.24) | data formatting | bytes 7340032 | tf_op jit(solution)/shard_map/reshape | solution.py:148
  306.7 16.0 %fusion.7 = bf16[512,3584]{1,0:T(8,128)(2,1)} fusion(bf16[1,1024,3584]{2,1,0:T(8,128)(2,1)} %param.31, bf16[512,3584]{1,0:T(8,128)(2,1)} %reshape.437, bf16[1,3584,1024]{2,1,0:T(8,128)(2,1)} %param.30), kind=kOutput, calls=%fused_computation.21 | convolution fusion | flops 7520649216 | bytes 22020096 | tf_op jit(solution)/shard_map/dot_general | solution.py:153
  322.7 7.0 %reshape.438 = bf16[128,4,3584]{2,1,0:T(4,128)(2,1)} reshape(bf16[512,3584]{1,0:T(8,128)(2,1)} %fusion.7) | data formatting | bytes 7340032 | tf_op jit(solution)/shard_map/reshape | solution.py:157
  329.7 5.1 %all-to-all-start.2 = ((bf16[128,4,3584]{2,1,0:T(4,128)(2,1)}), bf16[128,4,3584]{2,1,0:T(4,128)(2,1)}, u32[]{:S(2)}, u32[]{:S(2)}) async-start(bf16[128,4,3584]{2,1,0:T(4,128)(2,1)} %reshape.438), calls=%async_computation.4 | async-start | bytes 7340032 | tf_op jit(solution)/shard_map/all_to_all | solution.py:156
  334.9 0.6 pad_clamp_fusion
  335.5 0.9 reshape.433
  336.4 44.9 %all-to-all-done.2 = bf16[128,4,3584]{2,1,0:T(4,128)(2,1)} async-done(((bf16[128,4,3584]{2,1,0:T(4,128)(2,1)}), bf16[128,4,3584]{2,1,0:T(4,128)(2,1)}, u32[]{:S(2)}, u32[]{:S(2)}) %all-to-all-start.2) | async-done | bytes 3670048 | tf_op jit(solution)/shard_map/all_to_all | solution.py:156
  381.3 6.7 %reshape.439 = bf16[512,3584]{1,0:T(8,128)(2,1)} reshape(bf16[128,4,3584]{2,1,0:T(4,128)(2,1)} %all-to-all-done.2) | data formatting | bytes 7340032 | tf_op jit(solution)/shard_map/reshape | solution.py:164
  388.0 7.6 %gather_fusion.5 = bf16[256,3584]{1,0:T(8,128)(2,1)} fusion(bf16[512,3584]{1,0:T(8,128)(2,1)} %reshape.439, s32[1024]{0:T(1024)} %pad_clamp_fusion), kind=kCustom, calls=%fused_computation.5 | custom fusion | bytes 3671040 | tf_op jit(solution)/shard_map/gather | solution.py:164
  395.6 3.0 fusion.11
  398.6 1.8 add_convert_fusion
  400.4 1.8 reshape.440
  (70 shorter events, 2.2 us)
Async XLA Ops:
  7.2 4.4 %copy-start = (bf16[48,36864]{1,0:T(8,128)(2,1)S(1)}, bf16[48,36864]{1,0:T(8,128)(2,1)}, u32[]{:S(2)}) copy-start(bf16[48,36864]{1,0:T(8,128)(2,1)} %param.16) | copy-start | bytes 10616836
  7.2 200.2 %reduce-scatter.3.cloned.1.call-start = ((), (), s32[]{:S(2)}) async-start(), calls=%async_computation.5 | async-start | bytes 4587520 | tf_op jit(solution)/shard_map/reduce_scatter | solution.py:35
  36.7 3.4 copy-start.12
  57.2 1.4 copy-start.3
  57.3 1.5 copy-start.13
  57.3 1.7 copy-start.10
  58.7 2.4 copy-start.8
  58.8 6.3 %copy-start.14 = (s32[1,2]{1,0:T(1,128)S(1)}, s32[1,2]{1,0:T(1,128)}, u32[]{:S(2)}) copy-start(s32[1,2]{1,0:T(1,128)} %param.23) | copy-start | bytes 28
  62.1 9.8 %collective-permute-start = (bf16[2,145408]{1,0:T(2,128)(2,1)S(1)}, bf16[2,145408]{1,0:T(2,128)(2,1)S(1)}, u32[]{:S(2)}, u32[]{:S(2)}) collective-permute-start(bf16[2,145408]{1,0:T(2,128)(2,1)S(1)} %constant_dynamic-update-slice_fusion), channel_id=1, source_target_pairs={{0,16},{16,32},{32,48},{48,64},{64,80},{80,96},{96,112},{112,0},{1... | collective-permute-start | bytes 1744904 | tf_op jit(solution)/shard_map/ppermute | solution.py:29
  72.6 13.3 %collective-permute-start.1 = (bf16[2,145408]{1,0:T(2,128)(2,1)S(1)}, bf16[2,145408]{1,0:T(2,128)(2,1)S(1)}, u32[]{:S(2)}, u32[]{:S(2)}) collective-permute-start(bf16[2,145408]{1,0:T(2,128)(2,1)S(1)} %broadcast_select_fusion), channel_id=1, source_target_pairs={{0,32},{16,48},{32,64},{48,80},{64,96},{80,112},{96,0},{112,16},{1... | collective-permute-start | bytes 1744904 | tf_op jit(solution)/shard_map/ppermute | solution.py:29
  86.9 14.0 %collective-permute-start.2 = (bf16[2,145408]{1,0:T(2,128)(2,1)S(1)}, bf16[2,145408]{1,0:T(2,128)(2,1)}, u32[]{:S(2)}, u32[]{:S(2)}) collective-permute-start(bf16[2,145408]{1,0:T(2,128)(2,1)S(1)} %broadcast_select_fusion.1), channel_id=1, source_target_pairs={{0,64},{16,80},{32,96},{48,112},{64,0},{80,16},{96,32},{112,48},{1... | collective-permute-start | bytes 1744904 | tf_op jit(solution)/shard_map/ppermute | solution.py:29
  102.8 0.8 copy-start.7
  121.3 33.4 %copy-start.15 = (bf16[4,512,128]{2,1,0:T(8,128)(2,1)S(1)}, bf16[4,512,128]{2,1,0:T(8,128)(2,1)}, u32[]{:S(2)}) copy-start(bf16[4,512,128]{2,1,0:T(8,128)(2,1)} %param.28) | copy-start | bytes 1572868
  154.7 2.7 copy-start.5
  161.3 0.7 copy-start.2
  161.3 70.3 %reduce-scatter.5.cloned.1.call-start = ((), (), s32[]{:S(2)}) async-start(), calls=%async_computation.6 | async-start | bytes 1146880 | tf_op jit(solution)/shard_map/reduce_scatter | solution.py:35
  161.9 70.7 %copy-start.9 = (f32[3584]{0:T(1024)S(1)}, f32[3584]{0:T(1024)}, u32[]{:S(2)}) copy-start(f32[3584]{0:T(1024)} %param.27) | copy-start | bytes 43012
  207.7 36.0 %copy-start.4 = (f32[32,3584]{1,0:T(8,128)}, f32[32,3584]{1,0:T(8,128)S(1)}, u32[]{:S(2)}) copy-start(f32[32,3584]{1,0:T(8,128)S(1)} %reshape.441) | copy-start | bytes 1376260
  329.7 5.1 %copy-start.11 = (f32[32,8]{0,1:T(8,128)S(1)}, f32[32,8]{0,1:T(8,128)}, u32[]{:S(2)}) copy-start(f32[32,8]{0,1:T(8,128)} %param.25) | copy-start | bytes 3076
  329.7 5.8 %copy-start.6 = (bf16[32,3584]{1,0:T(8,128)(2,1)S(1)}, bf16[32,3584]{1,0:T(8,128)(2,1)}, u32[]{:S(2)}) copy-start(bf16[32,3584]{1,0:T(8,128)(2,1)} %reduce-scatter.5.cloned.1.call-done) | copy-start | bytes 688132
  329.7 51.6 %all-to-all-start.2 = ((bf16[128,4,3584]{2,1,0:T(4,128)(2,1)}), bf16[128,4,3584]{2,1,0:T(4,128)(2,1)}, u32[]{:S(2)}, u32[]{:S(2)}) async-start(bf16[128,4,3584]{2,1,0:T(4,128)(2,1)} %reshape.438), calls=%async_computation.4 | async-start | bytes 7340032 | tf_op jit(solution)/shard_map/all_to_all | solution.py:156
  388.0 14.2 %copy-start.1 = (bf16[48,36864]{1,0:T(8,128)(2,1)S(1)}, bf16[48,36864]{1,0:T(8,128)(2,1)}, u32[]{:S(2)}) copy-start(bf16[48,36864]{1,0:T(8,128)(2,1)} %param.16) | copy-start | bytes 10616836
Sparse Core Ops, SparseCore 0:
  161.4 45.9 reduce-scatter.2
  209.8 21.6 reduce-scatter.4
where the time goes:
time: 415 us; the launch traced here: 409 us
  waiting for transfers between devices  134 us (32%)
  local copies, waits for them, and re-layouts  93.2 us (22%)
  blocking collectives  87 us (21%)
  matrix products  43.5 us (10%)
  other arithmetic  23.2 us (6%)
  between operations  14.6 us (4%)
  starting transfers between devices  13.5 us (3%)
    reduce_scatter x2, waiting for transfers between devices, own_rows_2(): so_far = lax.psum_scatter(so_far, axis, scatter_dimension=0, tiled=True)  64.6 us
    all_to_all x1, blocking collectives, per_device(): lax.all_to_all(outgoing_tokens.reshape(device_count, capacity, D), REP_EP...  56.3 us
    all_to_all x1, waiting for transfers between devices, per_device(): lax.all_to_all(outer_out.reshape(device_count, capacity, D), REP_EP, spli...  44.9 us
    all_to_all x1, blocking collectives, per_device(): lax.all_to_all(token_latent, EP, split_axis=1, concat_axis=0, tiled=True)  30.6 us
    ppermute x3, waiting for transfers between devices, shifted(): return lax.ppermute(value, axis, pairs)  24.8 us
    dot_general x1, matrix products, per_device(): jnp.dot(inner_act, expert_out[0], preferred_element_type=jnp.float32)  16 us
    another operation x1, local copies, waits for them, and re-layouts, attend(): key_rows = key_block.reshape(request_count, MAXP * PAGE, KVW)  14.3 us
    sub x1, matrix products, attend(): exponent = jnp.exp(scores - jnp.max(scores, axis=2, keepdims=True))  10.7 us
  transfers between devices with their start and end apart: 6, of which 6 were waited for; matrix products, arithmetic and copies ran while one was open for 3% of the time, Pallas kernels for 0%

commit v1 on v0

--- a/solution.py
+++ b/solution.py
@@ -96,18 +96,10 @@
     matches = own_sheds[None, :] == jnp.arange(REQ_DEV, dtype=jnp.int32)[:, None]
     present = jnp.any(matches, axis=1)
     picker = jnp.argmax(matches, axis=1)
-    latent_width = SPEC * HEADS * LAT
     own_latent = attend(own_keys, queries, own_lengths)
-    arrived = jnp.concatenate((own_latent[own_sheds], residual[own_sheds]), axis=1)
-    for bit_level in range(rep_count.bit_length() - 1):
-        moved = shifted(arrived, "rep", 1 << bit_level)
-        taking = shifts // (1 << bit_level) % 2 == 1
-        arrived = jnp.where(taking[:, None], moved, arrived)
-    latent_all = fill_slots(arrived[:, :latent_width], picker, present, own_latent)
-    served_rest = fill_slots(arrived[:, latent_width:], picker, present, residual)
     tokens_dev = REQ_DEV * SPEC
     heads_dev = value_up.shape[0]
-    token_latent = latent_all.reshape(tokens_dev, HEADS * LAT)
+    token_latent = own_latent.reshape(tokens_dev, HEADS * LAT)
     regrouped = lax.all_to_all(token_latent, EP, split_axis=1, concat_axis=0, tiled=True)
     row_block = regrouped.reshape(tokens_dev * lax.axis_size(EP), heads_dev, LAT)
     lifted = jnp.einsum(
@@ -121,6 +113,15 @@
         ),
         EP,
     )
+    own_branch = branch.astype(jnp.bfloat16).reshape(REQ_DEV, SPEC * D)
+    arrived = jnp.concatenate((own_branch[own_sheds], residual[own_sheds]), axis=1)
+    for bit_level in range(rep_count.bit_length() - 1):
+        moved = shifted(arrived, "rep", 1 << bit_level)
+        taking = shifts // (1 << bit_level) % 2 == 1
+        arrived = jnp.where(taking[:, None], moved, arrived)
+    served_branch = fill_slots(arrived[:, : SPEC * D], picker, present, own_branch)
+    served_rest = fill_slots(arrived[:, SPEC * D :], picker, present, residual)
+    branch = served_branch.reshape(tokens_dev, D).astype(jnp.float32)
     mixed = served_rest.reshape(tokens_dev, D).astype(jnp.float32) + branch
     square = jnp.mean(mixed * mixed, axis=1, keepdims=True)
     normed = (mixed * lax.rsqrt(square + NORM_EPS) * norm_gain).astype(jnp.bfloat16)
@@ -166,7 +167,7 @@
         .astype(jnp.float32)
     )
     moe_sum = jnp.sum(gate_weight[:, :, None] * picked, axis=1)
-    attn_proj = branch.astype(jnp.bfloat16).reshape(REQ_DEV, SPEC * D)
+    attn_proj = served_branch
     layer_out = (mixed + moe_sum).astype(jnp.bfloat16).reshape(REQ_DEV, SPEC * D)
     return (attn_proj, layer_out)
 

time: 415 us -> 376 us (0.906)
  waiting for transfers between devices: 134 us -> 117 us
  local copies, waits for them, and re-layouts: 93.2 us -> 82.9 us
  other arithmetic: 23.2 us -> 13 us
  blocking collectives: 87 us -> 91.4 us
    ppermute x3, waiting for transfers between devices: 24.8 us -> 8.63 us  [shifted(): return lax.ppermute(value, axis, pairs)]
    gather x5 -> x3, local copies, waits for them, and re-layouts: 9.32 us -> 1.57 us  [fill_slots(): return jnp.where(present[:, None], arrived[picker], own_rows)]
    select_n x2 -> x1, other arithmetic: 6.05 us -> 0.01 us  [fill_slots(): return jnp.where(present[:, None], arrived[picker], own_rows)]
    all_to_all x0 -> x2, local copies, waits for them, and re-layouts: none -> 4.25 us  [per_device(): lax.all_to_all(token_latent, EP, split_axis=1, concat_axis=0, tiled=True)]
  transfers between devices with their start and end apart: 6 -> 6, of which waited for: 6 -> 6; matrix products, arithmetic and copies ran while one was open for 3% -> 1% of each run, Pallas kernels for 0% -> 0%
where the time goes in v1:
time: 376 us; the launch traced here: 374 us
  waiting for transfers between devices  117 us (31%)
  blocking collectives  91.4 us (24%)
  local copies, waits for them, and re-layouts  82.9 us (22%)
  matrix products  43.9 us (12%)
  between operations  14.3 us (4%)
  other arithmetic  13 us (3%)
  starting transfers between devices  11.2 us (3%)
    reduce_scatter x2, waiting for transfers between devices, own_rows_2(): so_far = lax.psum_scatter(so_far, axis, scatter_dimension=0, tiled=True)  63.1 us
    all_to_all x1, blocking collectives, per_device(): lax.all_to_all(outgoing_tokens.reshape(device_count, capacity, D), REP_EP...  56.8 us
    all_to_all x1, waiting for transfers between devices, per_device(): lax.all_to_all(outer_out.reshape(device_count, capacity, D), REP_EP, spli...  45.6 us
    all_to_all x1, blocking collectives, per_device(): lax.all_to_all(token_latent, EP, split_axis=1, concat_axis=0, tiled=True)  34.7 us
    dot_general x1, matrix products, per_device(): jnp.dot(inner_act, expert_out[0], preferred_element_type=jnp.float32)  16 us
    another operation x1, local copies, waits for them, and re-layouts, attend(): key_rows = key_block.reshape(request_count, MAXP * PAGE, KVW)  14.2 us
    sub x1, matrix products, attend(): exponent = jnp.exp(scores - jnp.max(scores, axis=2, keepdims=True))  10.7 us
    ppermute x3, waiting for transfers between devices, shifted(): return lax.ppermute(value, axis, pairs)  8.63 us
  transfers between devices with their start and end apart: 6, of which 6 were waited for; matrix products, arithmetic and copies ran while one was open for 1% of the time, Pallas kernels for 0%

profile of v1, /device:TPU:1, one launch (start us, length us, event | category | flops | bytes accessed | tf_op | source)
XLA Modules:
  0.0 374.2 jit_solution(15845066801113839272)
XLA Ops:
  7.2 0.6 and_select_fusion
  7.8 1.6 fusion.45
  9.3 0.2 reduce-window.18
  9.5 0.7 bitcast_subtract_fusion.1
  10.4 1.6 gather_fusion
  12.0 0.7 reshape.439
  12.7 0.8 copy.40
  13.5 0.7 reshape.420
  14.1 0.7 compare_select_fusion.3
  14.8 0.7 pad_clamp_fusion.1
  15.5 8.1 %gather_fusion.1 = bf16[96,36864]{1,0:T(8,128)(2,1)} fusion(bf16[48,36864]{1,0:T(8,128)(2,1)S(1)} %copy-done, s32[1024]{0:T(1024)S(1)} %get-tuple-element.18), kind=kCustom, calls=%fused_computation.1 | custom fusion | bytes 14156160 | tf_op jit(solution)/shard_map/gather | solution.py:92
  23.6 14.2 %reshape_reshape.4 = bf16[8,768,576]{2,1,0:T(8,128)(2,1)} reshape(bf16[96,36864]{1,0:T(8,128)(2,1)} %gather_fusion.1) | data formatting | bytes 14155776 | tf_op jit(solution)/shard_map/reshape;reshape | solution.py:41
  37.8 2.7 reshape.501
  40.5 3.3 reshape.416
  43.9 10.7 %fusion.51 = (f32[8,256]{1,0:T(8,128)S(1)}, f32[8,256,768]{1,2,0:T(8,128)}) fusion(s32[8,256]{1,0:T(8,128)S(1)} %broadcast_add_fusion.1, bf16[8,768,576]{2,1,0:T(8,128)(2,1)} %reshape_reshape.4, bf16[8,256,576]{2,1,0:T(8,128)(2,1)} %reshape.416), kind=kOutput, calls=%fused_computation.115 | convolution fusion | flops 1819804416 | bytes 15745024 | tf_op jit(solution)/shard_map/sub | solution.py:52
  54.6 7.8 %fusion.18 = bf16[8,256,512]{2,1,0:T(8,128)(2,1)} fusion(bf16[8,768,576]{2,1,0:T(8,128)(2,1)} %reshape_reshape.4, f32[8,256,768]{1,2,0:T(8,128)} %get-tuple-element.16, f32[8,256]{1,0:T(8,128)S(1)} %get-tuple-element.15), kind=kOutput, calls=%fused_computation.32 | convolution fusion | flops 1614807040 | bytes 14688256 | tf_op jit(solution)/shard_map/rqk,rkl->rql/dot_general | solution.py:54
  62.4 3.1 all_to_all.18
  65.5 1.2 copy.36
  66.7 34.7 %all_to_all.26 = bf16[32,16,2048]{2,0,1:T(8,128)(2,1)S(1)} all-to-all(bf16[32,16,2048]{2,0,1:T(8,128)(2,1)S(1)} %copy.36), channel_id=1, replica_groups=mesh['rep'=8,'ep_0'=4,'ep_1'=4] {'ep_0','ep_1'}, dimensions={1} | all-to-all | bytes 4194304 | tf_op jit(solution)/shard_map/all_to_all | solution.py:103
  101.3 2.8 reshape.417
  104.1 2.6 fusion.23
  106.8 3.9 %convolution_convert_fusion.1 = bf16[512,3584]{1,0:T(8,128)(2,1)} fusion(bf16[512,512]{0,1:T(8,128)(2,1)S(1)} %bitcast.103, bf16[512,3584]{1,0:T(8,128)(2,1)S(1)} %copy-done.4), kind=kOutput, calls=%fused_computation.21 | convolution fusion | flops 1880883200 | bytes 7864320 | tf_op jit(solution)/shard_map/dot_general | solution.py:109
  110.7 43.1 %reduce-scatter.3.cloned.1.call-done = bf16[128,3584]{1,0:T(8,128)(2,1)} async-done(((bf16[512,3584]{1,0:T(8,128)(2,1)}), bf16[128,3584]{1,0:T(8,128)(2,1)}) %reduce-scatter.3.cloned.1.call-update) | async-done | bytes 917520 | tf_op jit(solution)/shard_map/reduce_scatter | solution.py:35
  153.9 0.2 dynamic-slice_reduce_fusion
  154.1 1.9 gather_fusion.6
  156.0 0.1 copy.41
  156.1 0.2 fusion.31
  156.4 0.2 fusion.33
  156.7 0.6 gather_fusion.3
  157.3 0.6 iota_reduce_fusion
  158.0 20.0 %reduce-scatter.5.cloned.1.call-done = bf16[32,3584]{1,0:T(8,128)(2,1)} async-done(((bf16[128,3584]{1,0:T(8,128)(2,1)}), bf16[32,3584]{1,0:T(8,128)(2,1)}) %reduce-scatter.5.cloned.1.call-update) | async-done | bytes 229392 | tf_op jit(solution)/shard_map/reduce_scatter | solution.py:35
  178.0 1.1 reshape.419
  179.1 0.6 gather_fusion.2
  179.9 3.2 collective-permute-start
  183.0 1.8 collective-permute-done
  184.8 0.2 broadcast_select_fusion
  185.0 1.4 collective-permute-start.1
  186.4 0.2 fusion.28
  186.6 3.3 collective-permute-done.1
  189.9 0.2 broadcast_select_fusion.1
  190.2 1.5 collective-permute-start.2
  191.8 0.1 broadcast_in_dim.75
  191.9 3.5 collective-permute-done.2
  195.4 0.2 broadcast_select_fusion.2
  195.7 0.7 gather_fusion.4
  196.4 0.7 gather_fusion.5
  197.1 0.2 gather.35
  197.3 0.8 select_convert_fusion
  198.1 0.1 reshape.427
  198.2 0.3 multiply_reduce_fusion
  198.5 3.0 convolution_convert_fusion
  201.6 7.0 %reshape.422 = bf16[128,4,3584]{2,1,0:T(4,128)(2,1)} reshape(bf16[512,3584]{1,0:T(8,128)(2,1)} %convolution_convert_fusion) | data formatting | bytes 7340032 | tf_op jit(solution)/shard_map/reshape | solution.py:141
  208.6 56.8 %all_to_all.27 = bf16[128,4,3584]{2,1,0:T(4,128)(2,1)} all-to-all(bf16[128,4,3584]{2,1,0:T(4,128)(2,1)} %reshape.422), channel_id=1, replica_groups=mesh['rep'=8,'ep_0'=4,'ep_1'=4] {'rep','ep_0','ep_1'}, dimensions={0} | all-to-all | bytes 7340032 | tf_op jit(solution)/shard_map/all_to_all | solution.py:140
  265.3 6.7 %reshape.423 = bf16[512,3584]{1,0:T(8,128)(2,1)} reshape(bf16[128,4,3584]{2,1,0:T(4,128)(2,1)} %all_to_all.27) | data formatting | bytes 7340032 | tf_op jit(solution)/shard_map/reshape | solution.py:149
  272.1 16.0 %fusion.7 = bf16[512,3584]{1,0:T(8,128)(2,1)} fusion(bf16[1,1024,3584]{2,1,0:T(8,128)(2,1)} %param.31, bf16[512,3584]{1,0:T(8,128)(2,1)} %reshape.423, bf16[1,3584,1024]{2,1,0:T(8,128)(2,1)} %param.30), kind=kOutput, calls=%fused_computation.19 | convolution fusion | flops 7520649216 | bytes 22020096 | tf_op jit(solution)/shard_map/dot_general | solution.py:154
  288.0 7.0 %reshape.424 = bf16[128,4,3584]{2,1,0:T(4,128)(2,1)} reshape(bf16[512,3584]{1,0:T(8,128)(2,1)} %fusion.7) | data formatting | bytes 7340032 | tf_op jit(solution)/shard_map/reshape | solution.py:158
  295.0 5.1 %all-to-all-start.2 = ((bf16[128,4,3584]{2,1,0:T(4,128)(2,1)}), bf16[128,4,3584]{2,1,0:T(4,128)(2,1)}, u32[]{:S(2)}, u32[]{:S(2)}) async-start(bf16[128,4,3584]{2,1,0:T(4,128)(2,1)} %reshape.424), calls=%async_computation.4 | async-start | bytes 7340032 | tf_op jit(solution)/shard_map/all_to_all | solution.py:157
  300.2 0.6 pad_clamp_fusion
  300.8 45.6 %all-to-all-done.2 = bf16[128,4,3584]{2,1,0:T(4,128)(2,1)} async-done(((bf16[128,4,3584]{2,1,0:T(4,128)(2,1)}), bf16[128,4,3584]{2,1,0:T(4,128)(2,1)}, u32[]{:S(2)}, u32[]{:S(2)}) %all-to-all-start.2) | async-done | bytes 3670048 | tf_op jit(solution)/shard_map/all_to_all | solution.py:157
  346.5 6.7 %reshape.425 = bf16[512,3584]{1,0:T(8,128)(2,1)} reshape(bf16[128,4,3584]{2,1,0:T(4,128)(2,1)} %all-to-all-done.2) | data formatting | bytes 7340032 | tf_op jit(solution)/shard_map/reshape | solution.py:165
  353.2 7.6 %gather_fusion.7 = bf16[256,3584]{1,0:T(8,128)(2,1)} fusion(bf16[512,3584]{1,0:T(8,128)(2,1)} %reshape.425, s32[1024]{0:T(1024)} %pad_clamp_fusion), kind=kCustom, calls=%fused_computation.7 | custom fusion | bytes 3671040 | tf_op jit(solution)/shard_map/gather | solution.py:165
  360.8 3.0 fusion.11
  363.7 1.8 add_convert_fusion
  365.5 1.8 reshape.426
  (59 shorter events, 1.2 us)
Async XLA Ops:
  7.2 8.3 %copy-start = (bf16[48,36864]{1,0:T(8,128)(2,1)S(1)}, bf16[48,36864]{1,0:T(8,128)(2,1)}, u32[]{:S(2)}) copy-start(bf16[48,36864]{1,0:T(8,128)(2,1)} %param.16) | copy-start | bytes 10616836
  7.2 146.7 %reduce-scatter.3.cloned.1.call-start = ((), (), s32[]{:S(2)}) async-start(), calls=%async_computation.5 | async-start | bytes 4587520 | tf_op jit(solution)/shard_map/reduce_scatter | solution.py:35
  40.5 3.4 copy-start.9
  40.5 3.4 copy-start.10
  66.7 37.4 %copy-start.13 = (bf16[4,512,128]{2,1,0:T(8,128)(2,1)S(1)}, bf16[4,512,128]{2,1,0:T(8,128)(2,1)}, u32[]{:S(2)}) copy-start(bf16[4,512,128]{2,1,0:T(8,128)(2,1)} %param.28) | copy-start | bytes 1572868
  104.1 2.7 copy-start.4
  110.7 43.3 %copy-start.11 = (s32[8,1,2]{0,2,1:T(2,128)S(1)}, s32[8,1,2]{0,2,1:T(2,128)}, u32[]{:S(2)}) copy-start(s32[8,1,2]{0,2,1:T(2,128)} %param.22) | copy-start | bytes 196
  110.7 43.4 %copy-start.2 = (s32[128]{0:T(128)S(1)}, s32[128]{0:T(128)}, u32[]{:S(2)}) copy-start(s32[128]{0:T(128)} %param.26) | copy-start | bytes 1540
  110.7 46.0 %copy-start.5 = (bf16[8,14336]{1,0:T(8,128)(2,1)S(1)}, bf16[8,14336]{1,0:T(8,128)(2,1)}, u32[]{:S(2)}) copy-start(bf16[8,14336]{1,0:T(8,128)(2,1)} %param.18) | copy-start | bytes 688132
  110.7 47.3 %copy-start.12 = (s32[1,2]{1,0:T(1,128)S(1)}, s32[1,2]{1,0:T(1,128)}, u32[]{:S(2)}) copy-start(s32[1,2]{1,0:T(1,128)} %param.23) | copy-start | bytes 28
  110.7 67.3 %reduce-scatter.5.cloned.1.call-start = ((), (), s32[]{:S(2)}) async-start(), calls=%async_computation.6 | async-start | bytes 1146880 | tf_op jit(solution)/shard_map/reduce_scatter | solution.py:35
  179.9 4.9 %collective-permute-start = (bf16[2,28672]{1,0:T(2,128)(2,1)S(1)}, bf16[2,28672]{1,0:T(2,128)(2,1)S(1)}, u32[]{:S(2)}, u32[]{:S(2)}) collective-permute-start(bf16[2,28672]{1,0:T(2,128)(2,1)S(1)} %constant_dynamic-update-slice_fusion), channel_id=1, source_target_pairs={{0,16},{16,32},{32,48},{48,64},{64,80},{80,96},{96,112},{112,0},{1... | collective-permute-start | bytes 344072 | tf_op jit(solution)/shard_map/ppermute | solution.py:29
  185.0 4.9 %collective-permute-start.1 = (bf16[2,28672]{1,0:T(2,128)(2,1)S(1)}, bf16[2,28672]{1,0:T(2,128)(2,1)S(1)}, u32[]{:S(2)}, u32[]{:S(2)}) collective-permute-start(bf16[2,28672]{1,0:T(2,128)(2,1)S(1)} %broadcast_select_fusion), channel_id=1, source_target_pairs={{0,32},{16,48},{32,64},{48,80},{64,96},{80,112},{96,0},{112,16},{1... | collective-permute-start | bytes 344072 | tf_op jit(solution)/shard_map/ppermute | solution.py:29
  190.2 5.2 %collective-permute-start.2 = (bf16[2,28672]{1,0:T(2,128)(2,1)S(1)}, bf16[2,28672]{1,0:T(2,128)(2,1)S(1)}, u32[]{:S(2)}, u32[]{:S(2)}) collective-permute-start(bf16[2,28672]{1,0:T(2,128)(2,1)S(1)} %broadcast_select_fusion.1), channel_id=1, source_target_pairs={{0,64},{16,80},{32,96},{48,112},{64,0},{80,16},{96,32},{112,48},{1... | collective-permute-start | bytes 344072 | tf_op jit(solution)/shard_map/ppermute | solution.py:29
  195.6 2.6 copy-start.6
  196.4 2.2 copy-start.7
  198.5 10.0 %copy-start.3 = (f32[32,3584]{1,0:T(8,128)}, f32[32,3584]{1,0:T(8,128)S(1)}, u32[]{:S(2)}) copy-start(f32[32,3584]{1,0:T(8,128)S(1)} %get-tuple-element.5) | copy-start | bytes 1376260
  295.0 5.1 %copy-start.8 = (f32[32,8]{0,1:T(8,128)S(1)}, f32[32,8]{0,1:T(8,128)}, u32[]{:S(2)}) copy-start(f32[32,8]{0,1:T(8,128)} %param.25) | copy-start | bytes 3076
  295.0 51.4 %all-to-all-start.2 = ((bf16[128,4,3584]{2,1,0:T(4,128)(2,1)}), bf16[128,4,3584]{2,1,0:T(4,128)(2,1)}, u32[]{:S(2)}, u32[]{:S(2)}) async-start(bf16[128,4,3584]{2,1,0:T(4,128)(2,1)} %reshape.424), calls=%async_computation.4 | async-start | bytes 7340032 | tf_op jit(solution)/shard_map/all_to_all | solution.py:157
  353.2 14.2 %copy-start.1 = (bf16[48,36864]{1,0:T(8,128)(2,1)S(1)}, bf16[48,36864]{1,0:T(8,128)(2,1)}, u32[]{:S(2)}) copy-start(bf16[48,36864]{1,0:T(8,128)(2,1)} %param.16) | copy-start | bytes 10616836
Sparse Core Ops, SparseCore 0:
  110.8 43.0 reduce-scatter.2
  156.3 21.6 reduce-scatter.4
